TPU v7x, 128 devices: a whole 4x4x4 slice. The times are simulated.
128 devices in a mesh: seq: 16 (over x_lo, z, core), head: 4 (over y), batch: 2 (over x_hi).
Axes of the slice: x: 4 (x_hi: 2, x_lo: 2; x = x_hi * 2 + x_lo), y: 4, z: 4, core: 2. Of those that a mesh axis runs over, the one named last changes fastest.
Arguments:
- tokens: bfloat16 [32768, 2048], P(('batch', 'seq')), parts along dimension 0, may hold values from -6 to 6
- neighbor_bank: bfloat16 [512, 256, 2048], P(('batch', 'seq')), parts along dimension 0, may hold values from -2100 to 2100
- slots: int32 [512], P(('batch', 'seq')), parts along dimension 0, may hold values from 0 to 15
- w_query: bfloat16 [2048, 2048], P('seq', 'head'), may hold values from -0.125 to 0.125
- w_key: bfloat16 [2048, 2048], P('seq', 'head'), may hold values from -0.125 to 0.125
- w_value: bfloat16 [2048, 2048], P('seq', 'head'), may hold values from -0.125 to 0.125
- w_out: bfloat16 [2048, 2048], P('head', 'seq'), may hold values from -0.125 to 0.125
Outputs:
- cross_out: bfloat16 [32768, 2048], P(('batch', 'seq'), 'head'), parts along dimension 0
There are 2 independent parts, one for each index of `batch`. A program takes and returns all parts, laid end to end along the dimension named above; an argument that names none is the same for every part. Nothing has to cross between parts.
Inputs may be any that keep to these rules, and one draw needn't show every extreme that they name: Entry c picks row c // 16 * 16 + slots[c] of neighbor_bank.
All inputs are finite; a program needn't handle non-finite values.
Results may differ from a plain program's by a relative error of at most 0.006.
The roundings to bfloat16 on the way count: a program that leaves them out, or rounds other values in their place, can miss the bound.
Values may be sent and summed in bfloat16 or wider, within the bound.
No kernel may reach another device: no remote copies, remote signals or barrier semaphores. Data moves between devices by JAX's collectives and lax.ppermute only.
A program may use at most 128 MiB of HBM per device.

v0:
```python
import math
import jax
import jax.numpy as jnp
from jax import lax
from jax.sharding import PartitionSpec as P

HEAD_DIM = 128


def passed_along(block, axis, distance):
    devices = range(lax.axis_size(axis))
    route = [(i - distance, i) for i in devices if i - distance in devices]
    return lax.ppermute(block, axis, route)


def side_by_side(arrays, axis, dim, along):
    ends, at = ([], 0)
    for a in arrays[:-1]:
        at += a.shape[along]
        ends.append(at)
    both = jnp.concatenate(arrays, axis=along)
    return tuple(jnp.split(lax.all_gather(both, axis, axis=dim, tiled=True), ends, axis=along))


def attend(query_blocks, key_blocks, value_blocks):
    scores = jnp.einsum(
        "cmhd,cnhd->chmn", query_blocks, key_blocks, preferred_element_type=jnp.float32
    ) / math.sqrt(HEAD_DIM)
    peak_score = jnp.max(scores, axis=-1, keepdims=True)
    exponent = jnp.exp(scores - peak_score)
    weights = (exponent / jnp.sum(exponent, axis=-1, keepdims=True)).astype(jnp.bfloat16)
    blended = jnp.einsum(
        "chmn,cnhd->cmhd", weights, value_blocks, preferred_element_type=jnp.float32
    ).astype(jnp.bfloat16)
    return blended.reshape(blended.shape[0] * blended.shape[1], blended.shape[2] * blended.shape[3])


def fold_rows(source, shard_rows):
    return jnp.dot(source, shard_rows, preferred_element_type=jnp.float32)


def local(tokens, neighbor_bank, slots, w_query, w_key, w_value, w_out):
    tok_rows, model_width = tokens.shape
    block_count = neighbor_bank.shape[0]
    neighbor_rows = neighbor_bank.shape[1]
    block_len = tok_rows // block_count
    local_width = w_query.shape[1]
    local_heads = local_width // HEAD_DIM
    hidden = tokens.astype(jnp.float32)
    normed = (hidden * lax.rsqrt(jnp.mean(hidden * hidden, axis=-1, keepdims=True) + 1e-06)).astype(
        jnp.bfloat16
    )
    retrieved = jnp.take(neighbor_bank, slots, axis=0)
    arrived = passed_along(retrieved[block_count - 1], "seq", 1)
    context = jnp.concatenate([arrived[None], retrieved[: block_count - 1]], axis=0)
    context_flat = context.reshape(block_count * neighbor_rows, model_width)
    shard_rows = side_by_side((w_query, w_key, w_value), "seq", 0, 1)
    query_sum = fold_rows(normed, shard_rows[0])
    key_sum = fold_rows(context_flat, shard_rows[1])
    value_sum = fold_rows(context_flat, shard_rows[2])
    query_blocks = query_sum.astype(jnp.bfloat16).reshape(
        block_count, block_len, local_heads, HEAD_DIM
    )
    key_blocks = key_sum.astype(jnp.bfloat16).reshape(
        block_count, neighbor_rows, local_heads, HEAD_DIM
    )
    value_blocks = value_sum.astype(jnp.bfloat16).reshape(
        block_count, neighbor_rows, local_heads, HEAD_DIM
    )
    attended = attend(query_blocks, key_blocks, value_blocks)
    every_head = lax.all_gather(attended, "head", axis=1, tiled=True)
    wide_rows = lax.all_gather(w_out, "seq", axis=1, tiled=True)
    own_columns = lax.all_to_all(wide_rows, "head", split_axis=1, concat_axis=0, tiled=True)
    return jnp.dot(every_head, own_columns, preferred_element_type=jnp.float32).astype(jnp.bfloat16)


def solution(mesh):
    in_specs = (
        P(("batch", "seq"), None),
        P(("batch", "seq"), None, None),
        P(("batch", "seq")),
        P("seq", "head"),
        P("seq", "head"),
        P("seq", "head"),
        P("head", "seq"),
    )
    out_specs = P(("batch", "seq"), "head")
    return jax.shard_map(local, mesh=mesh, in_specs=in_specs, out_specs=out_specs, check_vma=False)
```

profile of v0, /device:TPU:3, one launch (start us, length us, event | category | flops | bytes accessed | tf_op | source)
XLA Modules:
  0.0 214.9 jit_solution(9233872285534013376)
XLA Ops:
  6.5 1.8 pad_maximum_fusion.1
  9.1 13.1 %gather_fusion = bf16[16,256,2048]{2,1,0:T(8,128)(2,1)} fusion(bf16[16,256,2048]{2,1,0:T(8,128)(2,1)} %param.8, s32[1024]{0:T(1024)S(1)} %pad_clamp_fusion), kind=kCustom, calls=%fused_computation | custom fusion | bytes 33554496 | tf_op jit(solution)/shard_map/jit(_take)/gather | solution.py:53
  22.2 8.7 %broadcast_select_fusion = bf16[16,256,2048]{2,1,0:T(8,128)(2,1)S(1)} fusion(bf16[16,256,2048]{2,1,0:T(8,128)(2,1)} %gather_fusion, pred[16]{0:T(512)(128)(4,1)S(1)} %compare_and_fusion), kind=kLoop, calls=%fused_computation.3 | loop fusion | flops 8388608 | bytes 33554448 | tf_op jit(solution)/shard_map/jit(_take)/select_n | solution.py:53
  31.0 5.9 %copy-done = bf16[16,256,2048]{2,1,0:T(8,128)(2,1)} copy-done((bf16[16,256,2048]{2,1,0:T(8,128)(2,1)}, bf16[16,256,2048]{2,1,0:T(8,128)(2,1)S(1)}, u32[]{:S(2)}) %copy-start) | copy-done | bytes 16777240
  37.0 4.1 %collective-permute-start = (bf16[256,2048]{1,0:T(8,128)(2,1)S(1)}, bf16[256,2048]{1,0:T(8,128)(2,1)S(1)}, u32[]{:S(2)}, u32[]{:S(2)}) collective-permute-start(bf16[256,2048]{1,0:T(8,128)(2,1)S(1)} %slice_bitcast_fusion), channel_id=1, source_target_pairs={{0,8},{8,16},{16,24},{24,32},{32,40},{40,48},{48,56},{56,64},{64,7... | collective-permute-start | bytes 3145736 | tf_op jit(solution)/shard_map/ppermute | solution.py:13
  42.0 2.2 %copy-done.1 = bf16[1024,2048]{1,0:T(8,128)(2,1)S(1)} copy-done((bf16[1024,2048]{1,0:T(8,128)(2,1)S(1)}, bf16[1024,2048]{1,0:T(8,128)(2,1)}, u32[]{:S(2)}) %copy-start.1) | copy-done | bytes 4194328
  44.2 0.9 fusion.1
  45.1 16.4 %collective-permute-done = bf16[256,2048]{1,0:T(8,128)(2,1)S(1)} collective-permute-done((bf16[256,2048]{1,0:T(8,128)(2,1)S(1)}, bf16[256,2048]{1,0:T(8,128)(2,1)S(1)}, u32[]{:S(2)}, u32[]{:S(2)}) %collective-permute-start) | collective-permute-done | bytes 1048608 | tf_op jit(solution)/shard_map/ppermute | solution.py:13
  61.5 6.4 %pad_maximum_fusion = bf16[16,256,2048]{2,1,0:T(8,128)(2,1)} fusion(bf16[15,256,2048]{2,1,0:T(8,128)(2,1)S(1)} %slice-done, bf16[1,256,2048]{2,1,0:T(8,128)(2,1)S(1)} %bitcast.25), kind=kLoop, calls=%fused_computation.2 | loop fusion | flops 8388608 | bytes 33554432 | tf_op jit(solution)/shard_map/concatenate | solution.py:55
  68.0 14.5 %convolution_convert_fusion = bf16[4096,512]{1,0:T(8,128)(2,1)} fusion(bf16[4096,2048]{1,0:T(8,128)(2,1)} %bitcast.18, bf16[2048,1536]{1,0:T(8,128)(2,1)} %all-gather.4.cloned.1.call-done), kind=kOutput, calls=%fused_computation.8 | convolution fusion | flops 8592031744 | bytes 23068672 | tf_op jit(solution)/shard_map/dot_general | solution.py:39
  82.4 7.0 %reshape.36 = bf16[16,256,4,128]{3,2,1,0:T(4,128)(2,1)} reshape(bf16[4096,512]{1,0:T(8,128)(2,1)} %convolution_convert_fusion) | data formatting | bytes 8388608 | tf_op jit(solution)/shard_map/reshape | solution.py:64
  89.4 5.2 %fusion.21 = bf16[1024,512]{1,0:T(8,128)(2,1)S(1)} fusion(bf16[2048,1536]{1,0:T(8,128)(2,1)} %all-gather.4.cloned.1.call-done, bf16[1024,2048]{1,0:T(8,128)(2,1)} %param.7, f32[1024]{0:T(1024)S(1)} %add_rsqrt_fusion), kind=kOutput, calls=%fused_computation.26 | convolution fusion | flops 2154299392 | bytes 7344128 | tf_op jit(solution)/shard_map/dot_general | solution.py:39
  94.9 14.4 %convolution_convert_fusion.1 = bf16[4096,512]{1,0:T(8,128)(2,1)} fusion(bf16[4096,2048]{1,0:T(8,128)(2,1)} %bitcast.19, bf16[2048,1536]{1,0:T(8,128)(2,1)} %all-gather.4.cloned.1.call-done), kind=kOutput, calls=%fused_computation.9 | convolution fusion | flops 8592031744 | bytes 23068672 | tf_op jit(solution)/shard_map/dot_general | solution.py:39
  109.3 6.9 %reshape.34 = bf16[16,256,4,128]{3,2,1,0:T(4,128)(2,1)} reshape(bf16[4096,512]{1,0:T(8,128)(2,1)} %convolution_convert_fusion.1) | data formatting | bytes 8388608 | tf_op jit(solution)/shard_map/reshape | solution.py:67
  116.2 3.8 %fusion.7 = f32[16,4,64,256]{3,2,1,0:T(8,128)S(1)} fusion(bf16[16,256,4,128]{3,2,1,0:T(4,128)(2,1)} %reshape.36, bf16[16,64,4,128]{3,2,1,0:T(4,128)(2,1)S(1)} %reshape.35), kind=kOutput, calls=%fused_computation.13 | convolution fusion | flops 268435456 | bytes 9437184 | tf_op jit(solution)/shard_map/cmhd,cnhd->chmn/dot_general | solution.py:26
  120.0 2.0 copy-done.2
  122.0 1.6 fusion.38
  123.6 11.9 %fusion.26 = bf16[16,64,4,128]{3,1,2,0:T(8,128)(2,1)S(1)} fusion(bf16[16,256,4,128]{3,2,1,0:T(4,128)(2,1)} %reshape.34, f32[16,4,64]{2,1,0:T(4,128)S(1)} %fusion.38, f32[16,4,64,256]{3,2,1,0:T(8,128)} %copy-done.2), kind=kOutput, calls=%fused_computation.28 | convolution fusion | flops 274206976 | bytes 9453568 | tf_op jit(solution)/shard_map/chmn,cnhd->cmhd/dot_general | solution.py:32
  135.5 0.9 copy.18
  136.4 1.2 copy.33
  137.6 35.9 %all_to_all.19 = bf16[512,4,512]{0,2,1:T(8,128)(2,1)S(1)} all-to-all(bf16[512,4,512]{0,2,1:T(8,128)(2,1)} %bitcast.23), channel_id=1, replica_groups=mesh['seq'=16,'head'=4,'batch'=2] {'head'}, dimensions={1} | all-to-all | bytes 4194304 | tf_op jit(solution)/shard_map/all_to_all | solution.py:73
  173.5 2.4 %copy.20 = bf16[4,512,512]{2,1,0:T(8,128)(2,1)} copy(bf16[4,512,512]{1,2,0:T(8,128)(2,1)S(1)} %bitcast.20) | data formatting | bytes 4194304 | tf_op jit(solution)/shard_map/all_to_all | solution.py:73
  175.9 26.3 %all-gather.6.cloned.1.call-done = bf16[1024,2048]{1,0:T(8,128)(2,1)} async-done(((bf16[1024,512]{1,0:T(8,128)(2,1)}), bf16[1024,2048]{1,0:T(8,128)(2,1)}) %all-gather.6.cloned.1.call-update) | async-done | bytes 4194320 | tf_op jit(solution)/shard_map/all_gather | solution.py:71
  202.2 6.2 %convolution_convert_fusion.2 = bf16[1024,512]{1,0:T(8,128)(2,1)} fusion(bf16[1024,2048]{1,0:T(8,128)(2,1)} %all-gather.6.cloned.1.call-done, bf16[2048,512]{1,0:T(8,128)(2,1)} %bitcast.24), kind=kOutput, calls=%fused_computation.27 | convolution fusion | flops 2148007936 | bytes 7340032 | tf_op jit(solution)/shard_map/dot_general | solution.py:74
  (24 shorter events, 2.0 us)
Async XLA Ops:
  6.5 61.4 %all-gather.4.cloned.1.call-start = ((), (), s32[]{:S(2)}) async-start(), calls=%async_computation.1 | async-start | bytes 6684672 | tf_op jit(solution)/shard_map/all_gather | solution.py:22
  8.4 129.2 %all-gather.8.cloned.1.call-start = ((), (), s32[]{:S(2)}) async-start(), calls=%async_computation.3 | async-start | bytes 2228224 | tf_op jit(solution)/shard_map/all_gather | solution.py:72
  9.1 13.1 %copy-start.4 = (s32[16]{0:T(128)S(1)}, s32[16]{0:T(128)}, u32[]{:S(2)}) copy-start(s32[16]{0:T(128)} %param.9) | copy-start | bytes 196
  22.2 18.9 %copy-start.3 = (bf16[512,128]{1,0:T(8,128)(2,1)S(1)}, bf16[512,128]{1,0:T(8,128)(2,1)}, u32[]{:S(2)}) copy-start(bf16[512,128]{1,0:T(8,128)(2,1)} %param.13) | copy-start | bytes 393220
  31.0 5.9 %copy-start = (bf16[16,256,2048]{2,1,0:T(8,128)(2,1)}, bf16[16,256,2048]{2,1,0:T(8,128)(2,1)S(1)}, u32[]{:S(2)}) copy-start(bf16[16,256,2048]{2,1,0:T(8,128)(2,1)S(1)} %broadcast_select_fusion) | copy-start | bytes 50331652
  37.0 24.5 %collective-permute-start = (bf16[256,2048]{1,0:T(8,128)(2,1)S(1)}, bf16[256,2048]{1,0:T(8,128)(2,1)S(1)}, u32[]{:S(2)}, u32[]{:S(2)}) collective-permute-start(bf16[256,2048]{1,0:T(8,128)(2,1)S(1)} %slice_bitcast_fusion), channel_id=1, source_target_pairs={{0,8},{8,16},{16,24},{24,32},{32,40},{40,48},{48,56},{56,64},{64,7... | collective-permute-start | bytes 3145736 | tf_op jit(solution)/shard_map/ppermute | solution.py:13
  41.9 160.2 %all-gather.6.cloned.1.call-start = ((), (), s32[]{:S(2)}) async-start(), calls=%async_computation.2 | async-start | bytes 5242880 | tf_op jit(solution)/shard_map/all_gather | solution.py:71
  42.0 2.3 %copy-start.1 = (bf16[1024,2048]{1,0:T(8,128)(2,1)S(1)}, bf16[1024,2048]{1,0:T(8,128)(2,1)}, u32[]{:S(2)}) copy-start(bf16[1024,2048]{1,0:T(8,128)(2,1)} %param.7) | copy-start | bytes 12582916
  42.0 19.5 %slice-start = ((bf16[16,256,2048]{2,1,0:T(8,128)(2,1)}), bf16[15,256,2048]{2,1,0:T(8,128)(2,1)S(1)}, s32[]{:S(2)}) async-start(bf16[16,256,2048]{2,1,0:T(8,128)(2,1)} %copy-done), calls=%async_computation.4 | async-start | bytes 31457280 | tf_op jit(solution)/shard_map/slice | solution.py:55
  120.0 2.0 copy-start.2
Sparse Core Ops, SparseCore 0:
  9.0 46.2 all-gather.3
  57.0 37.4 all-gather.7
  137.7 64.4 all-gather.5
where the time goes:
time: 216 us; the launch traced here: 215 us
  matrix products  55.9 us (26%)
  waiting for transfers between devices  42.7 us (20%)
  local copies, waits for them, and re-layouts  42.7 us (20%)
  blocking collectives  35.9 us (17%)
  other arithmetic  20.2 us (9%)
  between operations  13.2 us (6%)
  starting transfers between devices  4.22 us (2%)
    all_to_all x1, blocking collectives, local(): lax.all_to_all(wide_rows, 'head', split_axis=1, concat_axis=0, tiled=True)  35.9 us
    dot_general x3, matrix products, fold_rows(): return jnp.dot(source, shard_rows, preferred_element_type=jnp.float32)  34.1 us
    all_gather x1, waiting for transfers between devices, local(): every_head = lax.all_gather(attended, 'head', axis=1, tiled=True)  26.3 us
    ppermute x1, waiting for transfers between devices, passed_along(): return lax.ppermute(block, axis, route)  16.4 us
    gather x1, local copies, waits for them, and re-layouts, local(): retrieved = jnp.take(neighbor_bank, slots, axis=0)  13.1 us
    unnamed x12, local copies, waits for them, and re-layouts  12.1 us
    dot_general x1, matrix products, attend(): jnp.einsum('chmn,cnhd->cmhd', weights, value_blocks, preferred_element_ty...  11.9 us
    select_n x2, other arithmetic, local(): retrieved = jnp.take(neighbor_bank, slots, axis=0)  9.4 us
  transfers between devices with their start and end apart: 4, of which 2 were waited for; matrix products, arithmetic and copies ran while one was open for 47% of the time, Pallas kernels for 0%

commit v1 on v0

--- a/solution.py
+++ b/solution.py
@@ -1,3 +1,4 @@
+import functools
 import math
 import jax
 import jax.numpy as jnp
@@ -5,6 +6,16 @@
 from jax.sharding import PartitionSpec as P
 
 HEAD_DIM = 128
+
+
+def derive_the_meshes(x0, across):
+    p_next = jnp.concatenate(
+        lax.all_to_all(jnp.stack(jnp.split(x0, lax.axis_size(across), 1), 0), across, 0, 0), 0
+    )
+    return p_next
+
+
+take_case_on = functools.partial(derive_the_meshes, across="head")
 
 
 def passed_along(block, axis, distance):
@@ -70,7 +81,7 @@
     attended = attend(query_blocks, key_blocks, value_blocks)
     every_head = lax.all_gather(attended, "head", axis=1, tiled=True)
     wide_rows = lax.all_gather(w_out, "seq", axis=1, tiled=True)
-    own_columns = lax.all_to_all(wide_rows, "head", split_axis=1, concat_axis=0, tiled=True)
+    own_columns = take_case_on(wide_rows)
     return jnp.dot(every_head, own_columns, preferred_element_type=jnp.float32).astype(jnp.bfloat16)
 
 

time: 216 us -> 217 us (level)
    all_to_all x1 -> x0, local copies, waits for them, and re-layouts: 2.36 us -> none  [local(): lax.all_to_all(wide_rows, 'head', split_axis=1, concat_axis=0, tiled=True)]
    unnamed x12 -> x9, local copies, waits for them, and re-layouts: 12.1 us -> 11.3 us
  transfers between devices with their start and end apart: 4 -> 4, of which waited for: 2 -> 2; matrix products, arithmetic and copies ran while one was open for 47% -> 46% of each run, Pallas kernels for 0% -> 0%
where the time goes in v1:
time: 217 us; the launch traced here: 216 us
  matrix products  55.3 us (25%)
  waiting for transfers between devices  44.2 us (20%)
  local copies, waits for them, and re-layouts  41.2 us (19%)
  blocking collectives  37.4 us (17%)
  other arithmetic  20.4 us (9%)
  between operations  13.2 us (6%)
  starting transfers between devices  4.2 us (2%)
    all_to_all x1, blocking collectives, derive_the_meshes(): lax.all_to_all(jnp.stack(jnp.split(x0, lax.axis_size(across), 1), 0), acr...  37.4 us
    dot_general x3, matrix products, fold_rows(): return jnp.dot(source, shard_rows, preferred_element_type=jnp.float32)  34.1 us
    all_gather x1, waiting for transfers between devices, local(): every_head = lax.all_gather(attended, 'head', axis=1, tiled=True)  27 us
    ppermute x1, waiting for transfers between devices, passed_along(): return lax.ppermute(block, axis, route)  17.2 us
    gather x1, local copies, waits for them, and re-layouts, local(): retrieved = jnp.take(neighbor_bank, slots, axis=0)  13.1 us
    dot_general x1, matrix products, attend(): jnp.einsum('chmn,cnhd->cmhd', weights, value_blocks, preferred_element_ty...  11.9 us
    unnamed x9, local copies, waits for them, and re-layouts  11.3 us
    select_n x2, other arithmetic, local(): retrieved = jnp.take(neighbor_bank, slots, axis=0)  9.38 us
  transfers between devices with their start and end apart: 4, of which 2 were waited for; matrix products, arithmetic and copies ran while one was open for 46% of the time, Pallas kernels for 0%

profile of v1, /device:TPU:3, one launch (start us, length us, event | category | flops | bytes accessed | tf_op | source)
XLA Modules:
  0.0 215.9 jit_solution(10270995641923392693)
XLA Ops:
  6.5 1.8 pad_maximum_fusion.2
  9.1 13.1 %gather_fusion = bf16[16,256,2048]{2,1,0:T(8,128)(2,1)} fusion(bf16[16,256,2048]{2,1,0:T(8,128)(2,1)} %param.8, s32[1024]{0:T(1024)S(1)} %pad_clamp_fusion), kind=kCustom, calls=%fused_computation | custom fusion | bytes 33554496 | tf_op jit(solution)/shard_map/jit(_take)/gather | solution.py:64
  22.2 8.7 %broadcast_select_fusion = bf16[16,256,2048]{2,1,0:T(8,128)(2,1)S(1)} fusion(bf16[16,256,2048]{2,1,0:T(8,128)(2,1)} %gather_fusion, pred[16]{0:T(512)(128)(4,1)S(1)} %compare_and_fusion), kind=kLoop, calls=%fused_computation.3 | loop fusion | flops 8388608 | bytes 33554448 | tf_op jit(solution)/shard_map/jit(_take)/select_n | solution.py:64
  31.0 5.9 %copy-done = bf16[16,256,2048]{2,1,0:T(8,128)(2,1)} copy-done((bf16[16,256,2048]{2,1,0:T(8,128)(2,1)}, bf16[16,256,2048]{2,1,0:T(8,128)(2,1)S(1)}, u32[]{:S(2)}) %copy-start) | copy-done | bytes 16777240
  36.9 4.1 %collective-permute-start = (bf16[256,2048]{1,0:T(8,128)(2,1)S(1)}, bf16[256,2048]{1,0:T(8,128)(2,1)S(1)}, u32[]{:S(2)}, u32[]{:S(2)}) collective-permute-start(bf16[256,2048]{1,0:T(8,128)(2,1)S(1)} %slice_bitcast_fusion), channel_id=1, source_target_pairs={{0,8},{8,16},{16,24},{24,32},{32,40},{40,48},{48,56},{56,64},{64,7... | collective-permute-start | bytes 3145736 | tf_op jit(solution)/shard_map/ppermute | solution.py:24
  41.2 2.2 %copy-done.1 = bf16[1024,2048]{1,0:T(8,128)(2,1)S(1)} copy-done((bf16[1024,2048]{1,0:T(8,128)(2,1)S(1)}, bf16[1024,2048]{1,0:T(8,128)(2,1)}, u32[]{:S(2)}) %copy-start.1) | copy-done | bytes 4194328
  43.4 0.9 fusion.1
  44.3 17.2 %collective-permute-done = bf16[256,2048]{1,0:T(8,128)(2,1)S(1)} collective-permute-done((bf16[256,2048]{1,0:T(8,128)(2,1)S(1)}, bf16[256,2048]{1,0:T(8,128)(2,1)S(1)}, u32[]{:S(2)}, u32[]{:S(2)}) %collective-permute-start) | collective-permute-done | bytes 1048608 | tf_op jit(solution)/shard_map/ppermute | solution.py:24
  61.5 6.4 %pad_maximum_fusion = bf16[16,256,2048]{2,1,0:T(8,128)(2,1)} fusion(bf16[15,256,2048]{2,1,0:T(8,128)(2,1)S(1)} %slice-done, bf16[1,256,2048]{2,1,0:T(8,128)(2,1)S(1)} %bitcast.29), kind=kLoop, calls=%fused_computation.2 | loop fusion | flops 8388608 | bytes 33554432 | tf_op jit(solution)/shard_map/concatenate | solution.py:66
  68.0 14.5 %convolution_convert_fusion = bf16[4096,512]{1,0:T(8,128)(2,1)} fusion(bf16[4096,2048]{1,0:T(8,128)(2,1)} %bitcast.24, bf16[2048,1536]{1,0:T(8,128)(2,1)} %all-gather.4.cloned.1.call-done), kind=kOutput, calls=%fused_computation.8 | convolution fusion | flops 8592031744 | bytes 23068672 | tf_op jit(solution)/shard_map/dot_general | solution.py:50
  82.4 6.9 %reshape.36 = bf16[16,256,4,128]{3,2,1,0:T(4,128)(2,1)} reshape(bf16[4096,512]{1,0:T(8,128)(2,1)} %convolution_convert_fusion) | data formatting | bytes 8388608 | tf_op jit(solution)/shard_map/reshape | solution.py:75
  89.3 5.3 %fusion.21 = bf16[1024,512]{1,0:T(8,128)(2,1)S(1)} fusion(bf16[2048,1536]{1,0:T(8,128)(2,1)} %all-gather.4.cloned.1.call-done, bf16[1024,2048]{1,0:T(8,128)(2,1)} %param.7, f32[1024]{0:T(1024)S(1)} %add_rsqrt_fusion), kind=kOutput, calls=%fused_computation.27 | convolution fusion | flops 2154299392 | bytes 7344128 | tf_op jit(solution)/shard_map/dot_general | solution.py:50
  94.9 14.4 %convolution_convert_fusion.1 = bf16[4096,512]{1,0:T(8,128)(2,1)} fusion(bf16[4096,2048]{1,0:T(8,128)(2,1)} %bitcast.25, bf16[2048,1536]{1,0:T(8,128)(2,1)} %all-gather.4.cloned.1.call-done), kind=kOutput, calls=%fused_computation.9 | convolution fusion | flops 8592031744 | bytes 23068672 | tf_op jit(solution)/shard_map/dot_general | solution.py:50
  109.3 6.9 %reshape.34 = bf16[16,256,4,128]{3,2,1,0:T(4,128)(2,1)} reshape(bf16[4096,512]{1,0:T(8,128)(2,1)} %convolution_convert_fusion.1) | data formatting | bytes 8388608 | tf_op jit(solution)/shard_map/reshape | solution.py:78
  116.2 3.8 %fusion.7 = f32[16,4,64,256]{3,2,1,0:T(8,128)S(1)} fusion(bf16[16,256,4,128]{3,2,1,0:T(4,128)(2,1)} %reshape.36, bf16[16,64,4,128]{3,2,1,0:T(4,128)(2,1)S(1)} %reshape.35), kind=kOutput, calls=%fused_computation.13 | convolution fusion | flops 268435456 | bytes 9437184 | tf_op jit(solution)/shard_map/cmhd,cnhd->chmn/dot_general | solution.py:37
  119.9 2.0 copy-done.2
  121.9 1.6 fusion.38
  123.5 11.9 %fusion.26 = bf16[16,64,4,128]{3,1,2,0:T(8,128)(2,1)S(1)} fusion(bf16[16,256,4,128]{3,2,1,0:T(4,128)(2,1)} %reshape.34, f32[16,4,64]{2,1,0:T(4,128)S(1)} %fusion.38, f32[16,4,64,256]{3,2,1,0:T(8,128)} %copy-done.2), kind=kOutput, calls=%fused_computation.29 | convolution fusion | flops 274206976 | bytes 9453568 | tf_op jit(solution)/shard_map/chmn,cnhd->cmhd/dot_general | solution.py:43
  135.5 0.9 copy.14
  136.4 1.2 copy.27
  137.6 1.7 slice_bitcast_fusion.4
  139.5 37.4 %all_to_all.5 = bf16[4,512,512]{2,1,0:T(8,128)(2,1)S(1)} all-to-all(bf16[4,512,512]{2,1,0:T(8,128)(2,1)S(1)} %pad_maximum_fusion.1), channel_id=1, replica_groups=mesh['seq'=16,'head'=4,'batch'=2] {'head'}, dimensions={0} | all-to-all | bytes 4194304 | tf_op jit(solution)/shard_map/all_to_all | solution.py:13
  176.9 27.0 %all-gather.6.cloned.1.call-done = bf16[1024,2048]{1,0:T(8,128)(2,1)} async-done(((bf16[1024,512]{1,0:T(8,128)(2,1)}), bf16[1024,2048]{1,0:T(8,128)(2,1)}) %all-gather.6.cloned.1.call-update) | async-done | bytes 4194320 | tf_op jit(solution)/shard_map/all_gather | solution.py:82
  203.9 5.5 %convolution_convert_fusion.2 = bf16[1024,512]{1,0:T(8,128)(2,1)} fusion(bf16[1024,2048]{1,0:T(8,128)(2,1)} %all-gather.6.cloned.1.call-done, bf16[2048,512]{1,0:T(8,128)(2,1)S(1)} %bitcast.28), kind=kOutput, calls=%fused_computation.28 | convolution fusion | flops 2148007936 | bytes 7340032 | tf_op jit(solution)/shard_map/dot_general | solution.py:85
  (22 shorter events, 1.5 us)
Async XLA Ops:
  6.5 61.4 %all-gather.4.cloned.1.call-start = ((), (), s32[]{:S(2)}) async-start(), calls=%async_computation.1 | async-start | bytes 6684672 | tf_op jit(solution)/shard_map/all_gather | solution.py:33
  8.4 129.2 %all-gather.8.cloned.1.call-start = ((), (), s32[]{:S(2)}) async-start(), calls=%async_computation.3 | async-start | bytes 2228224 | tf_op jit(solution)/shard_map/all_gather | solution.py:83
  9.1 13.1 %copy-start.3 = (s32[16]{0:T(128)S(1)}, s32[16]{0:T(128)}, u32[]{:S(2)}) copy-start(s32[16]{0:T(128)} %param.9) | copy-start | bytes 196
  31.0 5.9 %copy-start = (bf16[16,256,2048]{2,1,0:T(8,128)(2,1)}, bf16[16,256,2048]{2,1,0:T(8,128)(2,1)S(1)}, u32[]{:S(2)}) copy-start(bf16[16,256,2048]{2,1,0:T(8,128)(2,1)S(1)} %broadcast_select_fusion) | copy-start | bytes 50331652
  36.9 24.6 %collective-permute-start = (bf16[256,2048]{1,0:T(8,128)(2,1)S(1)}, bf16[256,2048]{1,0:T(8,128)(2,1)S(1)}, u32[]{:S(2)}, u32[]{:S(2)}) collective-permute-start(bf16[256,2048]{1,0:T(8,128)(2,1)S(1)} %slice_bitcast_fusion), channel_id=1, source_target_pairs={{0,8},{8,16},{16,24},{24,32},{32,40},{40,48},{48,56},{56,64},{64,7... | collective-permute-start | bytes 3145736 | tf_op jit(solution)/shard_map/ppermute | solution.py:24
  41.1 162.8 %all-gather.6.cloned.1.call-start = ((), (), s32[]{:S(2)}) async-start(), calls=%async_computation.2 | async-start | bytes 5242880 | tf_op jit(solution)/shard_map/all_gather | solution.py:82
  41.1 2.3 %copy-start.1 = (bf16[1024,2048]{1,0:T(8,128)(2,1)S(1)}, bf16[1024,2048]{1,0:T(8,128)(2,1)}, u32[]{:S(2)}) copy-start(bf16[1024,2048]{1,0:T(8,128)(2,1)} %param.7) | copy-start | bytes 12582916
  41.2 20.4 %slice-start = ((bf16[16,256,2048]{2,1,0:T(8,128)(2,1)}), bf16[15,256,2048]{2,1,0:T(8,128)(2,1)S(1)}, s32[]{:S(2)}) async-start(bf16[16,256,2048]{2,1,0:T(8,128)(2,1)} %copy-done), calls=%async_computation.4 | async-start | bytes 31457280 | tf_op jit(solution)/shard_map/slice | solution.py:66
  119.9 2.0 copy-start.2
Sparse Core Ops, SparseCore 0:
  9.0 46.2 all-gather.3
  56.9 40.4 all-gather.7
  137.7 66.1 all-gather.5
